TPU v7x, 32 devices: a whole 2x2x4 slice. The times are simulated.
32 devices in a mesh: groups: 2 (over y), head: 4 (over z), state: 4 (over x, core).
Axes of the slice: x: 2, y: 2, z: 4, core: 2. Of those that a mesh axis runs over, the one named last changes fastest.
Arguments:
- tokens: bfloat16 [32, 2048], P(('groups', 'head'), 'state'), parts along dimension 0, may hold values from -20 to 20
- mixer_norm: float32 [2048], P('state'), may hold values from 0.1 to 1.9
- input_proj: bfloat16 [2, 2048, 8192], P(None, 'state', 'head'), may hold values from -0.125 to 0.125
- conv_weight: float32 [4, 8192], P(None, 'head'), may hold values from -3 to 3
- conv_bias: float32 [8192], P('head'), may hold values from -3 to 3
- conv_state: float32 [3, 32, 8192], P(None, 'groups', 'head'), parts along dimension 1, may hold values from -6 to 6
- state_proj: bfloat16 [8192, 288], P('head'), may hold values from -0.125 to 0.125
- step_gain: float32 [256], replicated, may hold values from 0.1 to 1.9
- step_proj: bfloat16 [256, 8192], P(None, 'head'), may hold values from -0.375 to 0.375
- step_bias: float32 [8192], P('head'), may hold values from -6 to -1
- decay_log: float32 [16, 8192], P('state', 'head'), may hold values from 0 to 2.77
- skip_gain: float32 [8192], P('head'), may hold values from 0.5 to 1.5
- ssm_state: float32 [16, 32, 8192], P('state', 'groups', 'head'), parts along dimension 1, may hold values from -6 to 6
- output_proj: bfloat16 [8192, 2048], P('head', 'state'), may hold values from -0.0625 to 0.0625
- moe_norm: float32 [2048], replicated, may hold values from 0.1 to 1.9
- router_weight: float32 [2048, 8], replicated, may hold values from -0.125 to 0.125
- expert_ids: int32 [32, 2], P(('groups', 'head')), parts along dimension 0, may hold values from 0 to 7, as said below
- slot_ids: int32 [32, 2], P(('groups', 'head')), parts along dimension 0, may hold values from 0 to 3, as said below
- gate_proj: bfloat16 [8, 2048, 7168], P('head', None, 'state'), may hold values from -0.125 to 0.125
- up_proj: bfloat16 [8, 2048, 7168], P('head', None, 'state'), may hold values from -0.125 to 0.125
- down_proj: bfloat16 [8, 7168, 2048], P('head', 'state'), may hold values from -0.0625 to 0.0625
Outputs:
- layer_out: bfloat16 [32, 2048], P(('groups', 'head'), 'state'), parts along dimension 0
- new_conv: float32 [3, 32, 8192], P(None, 'groups', 'head'), parts along dimension 1
- new_state: float32 [16, 32, 8192], P('state', 'groups', 'head'), parts along dimension 1
- expert_load: float32 [16], P('groups'), parts along dimension 0
- aux_loss: float32 [2], P('groups'), parts along dimension 0
There are 2 independent parts, one for each index of `groups`. A program takes and returns all parts, laid end to end along the dimension named above; an argument that names none is the same for every part. Nothing has to cross between parts.
Inputs may be any that keep to these rules, and one draw needn't show every extreme that they name: `expert_ids`: each row names 2 different experts. One expert, the same on every device, is named by every row. `slot_ids`: among the choices of one aligned block of 4 rows that name one expert, the slot positions are distinct and run from 0 to their count less one.
All inputs are finite; a program needn't handle non-finite values.
Results may differ from a plain program's by a relative error of at most 0.007.
Values may be sent and summed in bfloat16 or wider, within the bound.
A program may use at most 128 MiB of HBM per device.

v0:
```python
import jax
import jax.numpy as jnp
from jax import lax
from jax.sharding import PartitionSpec as P

D = 2048
D_STATE = 16
DT_RANK = 256
EXPERTS = 8
TOPK = 2
CAP = 2


NORM_EPS = 1e-05
STEP_EPS = 1e-06


def expert_ffn(received, gate_proj, up_proj, down_proj):
    gate_val = jnp.einsum("nlcd,ldf->nlcf", received, gate_proj, preferred_element_type=jnp.float32)
    up_val = jnp.einsum("nlcd,ldf->nlcf", received, up_proj, preferred_element_type=jnp.float32)
    hidden = (jax.nn.silu(gate_val) * up_val).astype(jnp.bfloat16)
    return jnp.einsum("nlcf,lfd->nlcd", hidden, down_proj, preferred_element_type=jnp.float32)


def per_device(
    tokens,
    mixer_norm,
    input_proj,
    conv_weight,
    conv_bias,
    conv_state,
    state_proj,
    step_gain,
    step_proj,
    step_bias,
    decay_log,
    skip_gain,
    ssm_state,
    output_proj,
    moe_norm,
    router_weight,
    expert_ids,
    slot_ids,
    gate_proj,
    up_proj,
    down_proj,
):
    head_count = lax.axis_size("head")
    state_index = lax.axis_index("state")
    own_rows = tokens.shape[0]
    tok_f32 = tokens.astype(jnp.float32)
    first_sq = lax.psum(jnp.sum(tok_f32 * tok_f32, axis=1), "state")
    inv_first = lax.rsqrt(first_sq / D + NORM_EPS)[:, None]
    normed = (tok_f32 * inv_first * mixer_norm).astype(jnp.bfloat16)
    branch_part = jnp.einsum(
        "td,kdc->ktc",
        lax.all_gather(normed, "head", axis=0, tiled=True),
        input_proj,
        preferred_element_type=jnp.float32,
    )
    branch_full = lax.psum(branch_part, "state")
    conv_input = branch_full[0]
    gate_branch = branch_full[1]
    window = jnp.concatenate([conv_state, conv_input[None]], axis=0)
    conv_out = jax.nn.silu(jnp.sum(conv_weight[:, None, :] * window, axis=0) + conv_bias)
    new_conv = window[1:]
    proj_part = jnp.dot(
        conv_out.astype(jnp.bfloat16), state_proj, preferred_element_type=jnp.float32
    )
    projected = lax.psum(proj_part, "head")
    step_low = projected[:, :DT_RANK]
    state_slab = decay_log.shape[0]
    b_input = lax.dynamic_slice_in_dim(projected, DT_RANK + state_index * state_slab, state_slab, 1)
    c_output = lax.dynamic_slice_in_dim(
        projected, DT_RANK + D_STATE + state_index * state_slab, state_slab, 1
    )
    step_inv = lax.rsqrt(jnp.mean(step_low * step_low, axis=1, keepdims=True) + STEP_EPS)
    step_normed = (step_low * step_inv * step_gain).astype(jnp.bfloat16)
    step_size = jax.nn.softplus(
        jnp.dot(step_normed, step_proj, preferred_element_type=jnp.float32) + step_bias
    )
    decay_rate = jnp.exp(-step_size[None] * jnp.exp(decay_log)[:, None, :])
    new_state = decay_rate * ssm_state + step_size[None] * b_input.T[:, :, None] * conv_out[None]
    read_part = jnp.sum(c_output.T[:, :, None] * new_state, axis=0)
    readout = lax.psum(read_part, "state")
    mixer_act = ((readout + skip_gain * conv_out) * jax.nn.silu(gate_branch)).astype(jnp.bfloat16)
    mixer_sum = lax.psum_scatter(
        jnp.dot(mixer_act, output_proj, preferred_element_type=jnp.float32),
        "head",
        scatter_dimension=0,
        tiled=True,
    )
    residual = (tok_f32 + mixer_sum).astype(jnp.bfloat16)
    full_rows = lax.all_gather(residual, "state", axis=1, tiled=True).astype(jnp.float32)
    inv_second = lax.rsqrt(jnp.mean(full_rows * full_rows, axis=1, keepdims=True) + NORM_EPS)
    scaled = full_rows * moe_norm
    logits = inv_second * jnp.dot(scaled, router_weight, precision=lax.Precision.HIGHEST)
    row_normed = (scaled * inv_second).astype(jnp.bfloat16)
    expert_hit = expert_ids[:, :, None] == jnp.arange(EXPERTS, dtype=jnp.int32)[None, None, :]
    chosen = jnp.sum(jnp.where(expert_hit, logits[:, None, :], 0.0), axis=2)
    gate_probs = jax.nn.sigmoid(chosen - chosen[:, ::-1])
    kept_mask = slot_ids < CAP
    mix_weight = jnp.where(kept_mask, gate_probs, 0.0)
    slot_hit = slot_ids[:, :, None] == jnp.arange(CAP, dtype=jnp.int32)[None, None, :]
    slot_place = expert_hit[:, :, :, None] & slot_hit[:, :, None, :]
    dispatch = jnp.sum(slot_place.astype(jnp.int32), axis=1).astype(jnp.bfloat16)
    combine_weight = jnp.sum(jnp.where(slot_place, mix_weight[:, :, None, None], 0.0), axis=1)
    outgoing = jnp.einsum(
        "tec,td->ecd", dispatch, row_normed, preferred_element_type=jnp.float32
    ).astype(jnp.bfloat16)
    row_width = outgoing.shape[2]
    local_experts = gate_proj.shape[0]
    expert_groups = EXPERTS // local_experts
    copies = head_count * local_experts // EXPERTS
    outgoing = jnp.broadcast_to(
        outgoing.reshape(expert_groups, 1, local_experts, CAP, row_width),
        (expert_groups, copies, local_experts, CAP, row_width),
    )
    outgoing = outgoing.reshape(head_count, local_experts, CAP, row_width)
    partial_out = expert_ffn(
        lax.all_to_all(outgoing, "head", split_axis=0, concat_axis=0, tiled=True),
        gate_proj,
        up_proj,
        down_proj,
    )
    returned = lax.all_to_all(
        partial_out.astype(jnp.bfloat16), "head", split_axis=0, concat_axis=0, tiled=True
    ).astype(partial_out.dtype)
    per_expert = returned.reshape(expert_groups, copies, local_experts, CAP, row_width).sum(axis=1)
    per_expert = per_expert.reshape(EXPERTS, CAP, row_width)
    expert_mix = jnp.einsum(
        "tec,ecd->td", combine_weight, per_expert, precision=lax.Precision.HIGHEST
    )
    expert_mix = lax.psum_scatter(
        expert_mix.astype(jnp.bfloat16), "state", scatter_dimension=1, tiled=True
    ).astype(jnp.float32)
    layer_out = (residual.astype(jnp.float32) + expert_mix).astype(jnp.bfloat16)
    load_own = jnp.sum(jnp.where(expert_hit & kept_mask[:, :, None], 1.0, 0.0), axis=(0, 1)).astype(
        jnp.float32
    )
    prob_own = jnp.sum(jax.nn.sigmoid(logits), axis=0)
    load_sum, prob_sum = lax.psum((load_own, prob_own), "head")
    total_rows = head_count * own_rows
    aux_value = EXPERTS * jnp.sum(load_sum / (total_rows * TOPK) * (prob_sum / total_rows))
    return (layer_out, new_conv, new_state, load_sum, aux_value.reshape(1))


def solution(mesh):
    return jax.shard_map(
        per_device,
        mesh=mesh,
        in_specs=(
            P(("groups", "head"), "state"),
            P("state"),
            P(None, "state", "head"),
            P(None, "head"),
            P("head"),
            P(None, "groups", "head"),
            P("head", None),
            P(),
            P(None, "head"),
            P("head"),
            P("state", "head"),
            P("head"),
            P("state", "groups", "head"),
            P("head", "state"),
            P(),
            P(),
            P(("groups", "head"), None),
            P(("groups", "head"), None),
            P("head", None, "state"),
            P("head", None, "state"),
            P("head", "state", None),
        ),
        out_specs=(
            P(("groups", "head"), "state"),
            P(None, "groups", "head"),
            P("state", "groups", "head"),
            P("groups"),
            P("groups"),
        ),
        check_vma=False,
    )
```

profile of v0, /device:TPU:0, one launch (start us, length us, event | category | flops | bytes accessed | tf_op | source)
XLA Modules:
  0.0 225.7 jit_solution(13633011839943154887)
XLA Ops:
  7.2 0.9 fusion.46
  8.2 8.4 %psum.42 = f32[4]{0:T(128)S(1)} all-reduce(f32[4]{0:T(128)S(1)} %fusion.46), channel_id=1, replica_groups=mesh['groups'=2,'head'=4,'state'=4] {'state'}, use_global_device_ids=true, to_apply=%region_1.0 | all-reduce | flops 4 | bytes 32 | tf_op jit(solution)/shard_map/psum | solution.py:52
  16.6 0.8 fusion.52
  17.4 13.4 %all-gather = bf16[4,4,512]{2,1,0:T(4,128)(2,1)S(1)} all-gather(bf16[1,4,512]{2,1,0:T(4,128)(2,1)S(1)} %fusion.52), channel_id=1, replica_groups=mesh['groups'=2,'head'=4,'state'=4] {'head'}, dimensions={0}, use_global_device_ids=true | all-gather | bytes 20480 | tf_op jit(solution)/shard_map/all_gather | solution.py:57
  30.8 3.6 %convolution_bitcast_fusion = f32[2,16,2048]{2,1,0:T(8,128)} fusion(bf16[16,512,1]{1,0,2:T(8,128)(2,1)S(1)} %reshape.86, bf16[2,512,2048]{2,1,0:T(8,128)(2,1)} %param.23), kind=kOutput, calls=%fused_computation.6 | convolution fusion | flops 67108864 | bytes 4472832 | tf_op jit(solution)/shard_map/td,kdc->ktc/dot_general | solution.py:55
  34.4 0.8 iota_compare_fusion
  36.5 0.8 exp.33
  37.3 1.2 dynamic-slice
  39.3 27.6 %all-reduce.5.cloned.1.call-done = f32[2,16,2048]{2,1,0:T(8,128)} async-done(((f32[2,16,2048]{2,1,0:T(8,128)}), f32[2,16,2048]{2,1,0:T(8,128)}) %all-reduce.5.cloned.1.call-update) | async-done | bytes 262160 | tf_op jit(solution)/shard_map/psum | solution.py:61
  66.9 0.9 slice.16
  67.8 1.1 fusion.26
  69.6 1.7 fusion.31
  71.3 19.0 %psum.44 = f32[16,288]{1,0:T(8,128)S(1)} all-reduce(f32[16,288]{1,0:T(8,128)S(1)} %fusion.31), channel_id=1, replica_groups=mesh['groups'=2,'head'=4,'state'=4] {'head'}, use_global_device_ids=true, to_apply=%region_4.5 | all-reduce | flops 4608 | bytes 36864 | tf_op jit(solution)/shard_map/psum | solution.py:70
  90.7 1.5 fusion.56
  92.2 2.7 %multiply_reduce_fusion = (f32[16,2048]{1,0:T(8,128)}, f32[4,16,2048]{2,1,0:T(8,128)}) fusion(f32[4,16]{1,0:T(4,128)S(1)} %copy.53, f32[16,2048]{1,0:T(8,128)S(1)} %divide_multiply_fusion, f32[4,16]{1,0:T(4,128)S(1)} %copy.54, f32[16,2048]{1,0:T(8,128)S(1)} %get-tuple-element.14, f32[4,16,2048]{2,1,0:T(8,128)} %param.33, f32[4,2048]{1,0:T(4,128)S(1)} %exp.33, ...), kind=kLoop, calls=%fused_computation.23 | loop fusion | flops 884736 | bytes 1606144 | tf_op jit(solution)/shard_map/reduce_sum | solution.py:84
  94.9 1.7 fusion.27
  96.6 27.5 %all-reduce.7.cloned.1.call-done = f32[16,2048]{1,0:T(8,128)} async-done(((f32[16,2048]{1,0:T(8,128)}), f32[16,2048]{1,0:T(8,128)}) %all-reduce.7.cloned.1.call-update) | async-done | bytes 131088 | tf_op jit(solution)/shard_map/psum | solution.py:85
  124.1 1.3 fusion.28
  125.5 19.0 %all-reduce = f32[16,512]{1,0:T(8,128)S(1)} all-reduce(f32[16,512]{1,0:T(8,128)S(1)} %fusion.28), channel_id=2, replica_groups=mesh['groups'=2,'head'=4,'state'=4] {'head'}, use_global_device_ids=true, to_apply=%region_8.9.clone | all-reduce | flops 8192 | bytes 65536
  145.2 5.2 %all_gather.7 = bf16[4,2048]{1,0:T(4,128)(2,1)S(1)} all-gather(bf16[4,512]{1,0:T(4,128)(2,1)S(1)} %fusion.49), channel_id=1, replica_groups=mesh['groups'=2,'head'=4,'state'=4] {'state'}, dimensions={1}, use_global_device_ids=true | all-gather | bytes 20480 | tf_op jit(solution)/shard_map/all_gather | solution.py:94
  150.5 1.1 fusion.54
  151.6 0.9 convolution_convert_fusion
  153.2 3.3 %all-to-all-start = ((bf16[4,2,2,2048]{3,2,1,0:T(2,128)(2,1)}), bf16[4,2,2,2048]{3,2,1,0:T(2,128)(2,1)S(1)}, u32[]{:S(2)}, u32[]{:S(2)}) async-start(bf16[4,2,2,2048]{3,2,1,0:T(2,128)(2,1)} %bitcast.6), calls=%async_computation | async-start | bytes 131072 | tf_op jit(solution)/shard_map/all_to_all | solution.py:121
  156.7 12.1 %all-reduce.1 = (f32[8]{0:T(128)S(1)}, f32[8]{0:T(128)S(1)}) all-reduce(f32[8]{0:T(128)S(1)} %get-tuple-element.5, f32[8]{0:T(128)S(1)} %get-tuple-element.15), channel_id=1, replica_groups=mesh['groups'=2,'head'=4,'state'=4] {'head'}, use_global_device_ids=true, to_apply=%region_15.16 | all-reduce | flops 16 | bytes 128 | tf_op jit(solution)/shard_map/psum | solution.py:142
  168.9 7.5 %fusion.6 = f32[4,2,2,1792]{3,0,2,1:T(4,128)S(1)} fusion(bf16[2,2048,1792]{2,1,0:T(8,128)(2,1)} %param.39, bf16[4,2,2,2048]{3,2,1,0:T(2,128)(2,1)S(1)} %all-to-all-done), kind=kOutput, calls=%fused_computation.7 | convolution fusion | flops 117440512 | bytes 14860288 | tf_op jit(solution)/shard_map/nlcd,ldf->nlcf/dot_general | solution.py:19
  176.4 7.5 %fusion.15 = bf16[4,2,2,1792]{3,0,2,1:T(4,128)(2,1)S(1)} fusion(bf16[2,2048,1792]{2,1,0:T(8,128)(2,1)} %param.40, f32[4,2,2,1792]{3,0,2,1:T(4,128)S(1)} %fusion.6, bf16[4,2,2,2048]{3,2,1,0:T(2,128)(2,1)S(1)} %all-to-all-done), kind=kOutput, calls=%fused_computation.11 | convolution fusion | flops 117612544 | bytes 14917632 | tf_op jit(solution)/shard_map/nlcd,ldf->nlcf/dot_general | solution.py:20
  183.9 2.1 fusion.21
  186.7 3.3 %all-to-all-start.1 = ((bf16[4,2,2,2048]{3,2,1,0:T(2,128)(2,1)}), bf16[4,2,2,2048]{3,2,1,0:T(2,128)(2,1)S(1)}, u32[]{:S(2)}, u32[]{:S(2)}) async-start(bf16[4,2,2,2048]{3,2,1,0:T(2,128)(2,1)} %copy.58), calls=%async_computation.1 | async-start | bytes 131072 | tf_op jit(solution)/shard_map/all_to_all | solution.py:126
  190.1 5.6 %all-to-all-done.1 = bf16[4,2,2,2048]{3,2,1,0:T(2,128)(2,1)S(1)} async-done(((bf16[4,2,2,2048]{3,2,1,0:T(2,128)(2,1)}), bf16[4,2,2,2048]{3,2,1,0:T(2,128)(2,1)S(1)}, u32[]{:S(2)}, u32[]{:S(2)}) %all-to-all-start.1) | async-done | bytes 65568 | tf_op jit(solution)/shard_map/all_to_all | solution.py:126
  196.0 1.1 copy.64
  198.3 18.1 %reduce-scatter.4.cloned.1.call-done = bf16[512,4]{1,0:T(8,128)(2,1)} async-done(((bf16[2048,4]{1,0:T(8,128)(2,1)}), bf16[512,4]{1,0:T(8,128)(2,1)}) %reduce-scatter.4.cloned.1.call-update) | async-done | bytes 4112
  216.4 1.0 copy.65
  (47 shorter events, 6.8 us)
Async XLA Ops:
  7.2 117.0 %copy-start = (bf16[2048,512]{1,0:T(8,128)(2,1)S(1)}, bf16[2048,512]{1,0:T(8,128)(2,1)}, u32[]{:S(2)}) copy-start(bf16[2048,512]{1,0:T(8,128)(2,1)} %param.34) | copy-start | bytes 6291460
  7.2 149.4 %copy-start.1 = (s32[4,2]{0,1:T(2,128)S(1)}, s32[4,2]{0,1:T(2,128)}, u32[]{:S(2)}) copy-start(s32[4,2]{0,1:T(2,128)} %param.37) | copy-start | bytes 100
  7.2 149.5 %copy-start.2 = (s32[4,2]{0,1:T(2,128)S(1)}, s32[4,2]{0,1:T(2,128)}, u32[]{:S(2)}) copy-start(s32[4,2]{0,1:T(2,128)} %param.38) | copy-start | bytes 100
  7.2 59.7 %all-reduce.5.cloned.1.call-start = ((), (), s32[]{:S(2)}) async-start(), calls=%async_computation.3 | async-start | bytes 524288 | tf_op jit(solution)/shard_map/psum | solution.py:61
  34.4 89.8 %all-reduce.7.cloned.1.call-start = ((), (), s32[]{:S(2)}) async-start(), calls=%async_computation.4 | async-start | bytes 262144 | tf_op jit(solution)/shard_map/psum | solution.py:85
  153.2 15.7 %all-to-all-start = ((bf16[4,2,2,2048]{3,2,1,0:T(2,128)(2,1)}), bf16[4,2,2,2048]{3,2,1,0:T(2,128)(2,1)S(1)}, u32[]{:S(2)}, u32[]{:S(2)}) async-start(bf16[4,2,2,2048]{3,2,1,0:T(2,128)(2,1)} %bitcast.6), calls=%async_computation | async-start | bytes 131072 | tf_op jit(solution)/shard_map/all_to_all | solution.py:121
  168.9 28.1 %copy-start.3 = (f32[8]{0:T(128)}, f32[8]{0:T(128)S(1)}, u32[]{:S(2)}) copy-start(f32[8]{0:T(128)S(1)} %get-tuple-element.7) | copy-start | bytes 100
  168.9 15.0 %slice-start = ((s8[14680064]{0:T(1024)(128)(4,1)}), s8[4194304]{0:T(1024)(128)(4,1)S(1)}, s32[]{:S(2)}) async-start(s8[14680064]{0:T(1024)(128)(4,1)} %bitcast.71), calls=%async_computation.6 | async-start | bytes 8388608
  168.9 15.0 %slice-start.1 = ((s8[14680064]{0:T(1024)(128)(4,1)}), s8[4194304]{0:T(1024)(128)(4,1)S(1)}, s32[]{:S(2)}) async-start(s8[14680064]{0:T(1024)(128)(4,1)} %bitcast.71), calls=%async_computation.7 | async-start | bytes 8388608
  176.4 7.5 %slice-start.2 = ((s8[14680064]{0:T(1024)(128)(4,1)}), s8[4194304]{0:T(1024)(128)(4,1)S(1)}, s32[]{:S(2)}) async-start(s8[14680064]{0:T(1024)(128)(4,1)} %bitcast.71), calls=%async_computation.8 | async-start | bytes 8388608
  176.4 7.5 %slice-start.3 = ((s8[14680064]{0:T(1024)(128)(4,1)}), s8[2097152]{0:T(1024)(128)(4,1)S(1)}, s32[]{:S(2)}) async-start(s8[14680064]{0:T(1024)(128)(4,1)} %bitcast.71), calls=%async_computation.9 | async-start | bytes 4194304
  186.7 9.0 %all-to-all-start.1 = ((bf16[4,2,2,2048]{3,2,1,0:T(2,128)(2,1)}), bf16[4,2,2,2048]{3,2,1,0:T(2,128)(2,1)S(1)}, u32[]{:S(2)}, u32[]{:S(2)}) async-start(bf16[4,2,2,2048]{3,2,1,0:T(2,128)(2,1)} %copy.58), calls=%async_computation.1 | async-start | bytes 131072 | tf_op jit(solution)/shard_map/all_to_all | solution.py:126
  190.0 26.4 %reduce-scatter.4.cloned.1.call-start = ((), (), s32[]{:S(2)}) async-start(), calls=%async_computation.5 | async-start | bytes 655360
Sparse Core Ops, SparseCore 0:
  34.5 32.3 all-reduce.4
  95.0 29.0 all-reduce.6
  197.2 19.2 reduce-scatter.3
where the time goes:
time: 227 us; the launch traced here: 226 us
  waiting for transfers between devices  78.8 us (35%)
  blocking collectives  77.1 us (34%)
  matrix products  27.5 us (12%)
  between operations  16.4 us (7%)
  other arithmetic  12.6 us (6%)
  local copies, waits for them, and re-layouts  6.69 us (3%)
  starting transfers between devices  6.69 us (3%)
    psum x1, waiting for transfers between devices, per_device(): branch_full = lax.psum(branch_part, 'state')  27.6 us
    psum x1, waiting for transfers between devices, per_device(): readout = lax.psum(read_part, 'state')  27.5 us
    unnamed x1, blocking collectives  19 us
    psum x1, blocking collectives, per_device(): projected = lax.psum(proj_part, 'head')  19 us
    unnamed x4, waiting for transfers between devices  18.2 us
    all_gather x1, blocking collectives, per_device(): lax.all_gather(normed, 'head', axis=0, tiled=True)  13.4 us
    psum x1, blocking collectives, per_device(): load_sum, prob_sum = lax.psum((load_own, prob_own), 'head')  12.1 us
    psum x1, blocking collectives, per_device(): first_sq = lax.psum(jnp.sum(tok_f32 * tok_f32, axis=1), 'state')  8.36 us
  transfers between devices with their start and end apart: 5, of which 4 were waited for; matrix products, arithmetic and copies ran while one was open for 3% of the time, Pallas kernels for 0%

commit v1 on v0

--- a/solution.py
+++ b/solution.py
@@ -1,6 +1,8 @@
 import jax
 import jax.numpy as jnp
 from jax import lax
+from jax.experimental import pallas as pl
+from jax.experimental.pallas import tpu as pltpu
 from jax.sharding import PartitionSpec as P
 
 D = 2048
@@ -13,6 +15,7 @@
 
 NORM_EPS = 1e-05
 STEP_EPS = 1e-06
+VMEM_BYTES = 67043328
 
 
 def expert_ffn(received, gate_proj, up_proj, down_proj):
@@ -145,9 +148,370 @@
     return (layer_out, new_conv, new_state, load_sum, aux_value.reshape(1))
 
 
+def dot(left, right):
+    return jnp.dot(left, right, preferred_element_type=jnp.float32)
+
+
+def fused_kernel(dims, *refs):
+    heads, states, own, local, split, slab = dims
+    (pay, nrm, wi, cw, cb, cs, wsp, sg, wst, sb, dl, sk, ss, wo, mn, rw, wg, wu, wd) = refs[:19]
+    (out, new_conv, new_state, load, aux) = refs[19:24]
+    (v_nrm, v_wi, v_cw, v_cb, v_cs, v_wsp, v_sg, v_wst, v_sb, v_dl, v_sk, v_ss, v_wo, v_mn, v_rw, v_wg, v_wu, v_wd) = refs[24:42]
+    (pay_buf, sq_buf, br_buf, pj_buf, rd_buf, ms_buf, rs_buf, xo_buf, xi_buf) = refs[42:51]
+    (conv_in, conv_out, gate_act, resid, xn, hid, ld_sem, ex_sem, in_sem, h_send, h_recv, s_send, s_recv, x_send, x_recv, o_sem) = refs[51:]
+    me_h = lax.axis_index("head")
+    me_s = lax.axis_index("state")
+    batch = pay.shape[0]
+    width = v_nrm.shape[1]
+    model = width * states
+    chans = v_cb.shape[1]
+    rank = v_sg.shape[1]
+    experts = v_rw.shape[1]
+
+    smalls = [(nrm, v_nrm), (cw, v_cw), (cb, v_cb), (cs, v_cs), (wsp, v_wsp), (sg, v_sg), (wst, v_wst), (sb, v_sb), (dl, v_dl), (sk, v_sk), (ss, v_ss), (wo, v_wo), (mn, v_mn), (rw, v_rw)]
+    in_copies = [pltpu.make_async_copy(wi.at[k], v_wi.at[k], in_sem.at[k]) for k in range(2)]
+    loads = [pltpu.make_async_copy(a, b, ld_sem.at[i]) for i, (a, b) in enumerate(smalls)]
+    (l_nrm, l_cw, l_cb, l_cs, l_wsp, l_sg, l_wst, l_sb, l_dl, l_sk, l_ss, l_wo, l_mn, l_rw) = loads
+    ex_copies = []
+    for e in range(local):
+        ex_copies.append([pltpu.make_async_copy(a.at[e], b.at[e], ex_sem.at[3 * e + j]) for j, (a, b) in enumerate(((wg, v_wg), (wu, v_wu), (wd, v_wd)))])
+    l_nrm.start()
+    for c in in_copies:
+        c.start()
+    for c in loads[1:]:
+        c.start()
+
+    barrier = pltpu.get_barrier_semaphore()
+    for dh in range(heads):
+        for ds in range(states):
+            if dh or ds:
+                pl.semaphore_signal(
+                    barrier,
+                    inc=1,
+                    device_id={"head": lax.rem(me_h + dh, heads), "state": lax.rem(me_s + ds, states)},
+                    device_id_type=pl.DeviceIdType.MESH,
+                )
+    pl.semaphore_wait(barrier, heads * states - 1)
+
+    def head_send(step, source, dest):
+        copies = []
+        for d in range(1, heads):
+            c = pltpu.make_async_remote_copy(
+                src_ref=source,
+                dst_ref=dest,
+                send_sem=h_send.at[step, d],
+                recv_sem=h_recv.at[step, d],
+                device_id={"head": lax.rem(me_h + d, heads)},
+                device_id_type=pl.DeviceIdType.MESH,
+            )
+            c.start()
+            copies.append(c)
+        return copies
+
+    def state_send(step, source, dest):
+        copies = []
+        for d in range(1, states):
+            c = pltpu.make_async_remote_copy(
+                src_ref=source,
+                dst_ref=dest,
+                send_sem=s_send.at[step, d],
+                recv_sem=s_recv.at[step, d],
+                device_id={"state": lax.rem(me_s + d, states)},
+                device_id_type=pl.DeviceIdType.MESH,
+            )
+            c.start()
+            copies.append(c)
+        return copies
+
+    def recv(copies):
+        for c in copies:
+            c.wait_recv()
+
+    pending = []
+    c_pay = head_send(0, pay, pay_buf.at[me_h])
+    pending += c_pay
+    pay_buf[me_h] = pay[...]
+    for group in ex_copies:
+        for c in group:
+            c.start()
+    recv(c_pay)
+    whole = pay_buf[0].astype(jnp.float32)
+    for j in range(1, heads):
+        whole = whole + pay_buf[j].astype(jnp.float32)
+    tok = whole[:, :width]
+    route = whole[:, width:]
+    sq_buf[me_s] = jnp.broadcast_to(jnp.sum(tok * tok, axis=1, keepdims=True), sq_buf.shape[1:])
+    c_sq = state_send(0, sq_buf.at[me_s], sq_buf.at[me_s])
+    pending += c_sq
+    l_nrm.wait()
+    xm = (tok * v_nrm[...]).astype(jnp.bfloat16)
+    c_br = []
+    for k in range(2):
+        in_copies[k].wait()
+        br_buf[k, me_s] = dot(xm, v_wi[k]).astype(jnp.bfloat16)
+        c_br.append(state_send(1 + k, br_buf.at[k, me_s], br_buf.at[k, me_s]))
+        pending += c_br[k]
+    for c in loads[1:]:
+        c.wait()
+    recv(c_sq)
+    total = sq_buf[0]
+    for j in range(1, states):
+        total = total + sq_buf[j]
+    inv_first = lax.rsqrt(total[:, :1] / model + NORM_EPS)
+    recv(c_br[0])
+    block = min(512, chans)
+    for c0 in range(0, chans, block):
+        cols = pl.ds(c0, block)
+        value = br_buf[0, 0, :, cols].astype(jnp.float32)
+        for j in range(1, states):
+            value = value + br_buf[0, j, :, cols].astype(jnp.float32)
+        value = value * inv_first
+        conv_in[:, cols] = value
+        taps = v_cs.shape[0]
+        acc = v_cw[taps : taps + 1, cols] * value
+        for k in range(taps):
+            acc = acc + v_cw[k : k + 1, cols] * v_cs[k, :, cols]
+        acc = acc + v_cb[:, cols]
+        conv_out[:, cols] = acc / (1.0 + jnp.exp(-acc))
+    pj_buf[me_h] = dot(conv_out[...].astype(jnp.bfloat16), v_wsp[...])
+    c_pj = head_send(1, pj_buf.at[me_h], pj_buf.at[me_h])
+    pending += c_pj
+    out_copies = [pltpu.make_async_copy(conv_in, new_conv.at[v_cs.shape[0] - 1], o_sem.at[0])]
+    for k in range(1, v_cs.shape[0]):
+        out_copies.append(pltpu.make_async_copy(v_cs.at[k], new_conv.at[k - 1], o_sem.at[k]))
+    for c in out_copies:
+        c.start()
+    recv(c_br[1])
+    for c0 in range(0, chans, block):
+        cols = pl.ds(c0, block)
+        value = br_buf[1, 0, :, cols].astype(jnp.float32)
+        for j in range(1, states):
+            value = value + br_buf[1, j, :, cols].astype(jnp.float32)
+        value = value * inv_first
+        gate_act[:, cols] = value / (1.0 + jnp.exp(-value))
+    recv(c_pj)
+    projected = pj_buf[0]
+    for j in range(1, heads):
+        projected = projected + pj_buf[j]
+    step_low = projected[:, :rank]
+    step_inv = lax.rsqrt(jnp.mean(step_low * step_low, axis=1, keepdims=True) + STEP_EPS)
+    step_normed = (step_low * step_inv * v_sg[...]).astype(jnp.bfloat16)
+    tail = projected[:, rank:]
+    lane = lax.broadcasted_iota(jnp.int32, tail.shape, 1)
+    bs = []
+    ks = []
+    for n in range(slab):
+        at = me_s * slab + n
+        bs.append(jnp.sum(jnp.where(lane == at, tail, 0.0), axis=1, keepdims=True))
+        ks.append(jnp.sum(jnp.where(lane == at + slab * states, tail, 0.0), axis=1, keepdims=True))
+    for c0 in range(0, chans, block):
+        cols = pl.ds(c0, block)
+        raw = dot(step_normed, v_wst[:, cols]) + v_sb[:, cols]
+        step_size = jnp.maximum(raw, 0.0) + jnp.log1p(jnp.exp(-jnp.abs(raw)))
+        driven = step_size * conv_out[:, cols]
+        read = None
+        for n in range(slab):
+            decay = jnp.exp(-step_size * jnp.exp(v_dl[n : n + 1, cols]))
+            fresh = decay * v_ss[n, :, cols] + bs[n] * driven
+            v_ss[n, :, cols] = fresh
+            term = ks[n] * fresh
+            read = term if read is None else read + term
+        rd_buf[me_s, :, cols] = read.astype(jnp.bfloat16)
+    c_rd = state_send(3, rd_buf.at[me_s], rd_buf.at[me_s])
+    pending += c_rd
+    state_out = pltpu.make_async_copy(v_ss, new_state, o_sem.at[v_cs.shape[0]])
+    state_out.start()
+    out_copies.append(state_out)
+    recv(c_rd)
+    mixed = None
+    for c0 in range(0, chans, block):
+        cols = pl.ds(c0, block)
+        value = rd_buf[0, :, cols].astype(jnp.float32)
+        for j in range(1, states):
+            value = value + rd_buf[j, :, cols].astype(jnp.float32)
+        act = ((value + v_sk[:, cols] * conv_out[:, cols]) * gate_act[:, cols]).astype(jnp.bfloat16)
+        term = dot(act, v_wo[cols, :])
+        mixed = term if mixed is None else mixed + term
+    ms_buf[me_h] = mixed.astype(jnp.bfloat16)
+    c_ms = head_send(2, ms_buf.at[me_h], ms_buf.at[me_h])
+    pending += c_ms
+    recv(c_ms)
+    value = ms_buf[0].astype(jnp.float32)
+    for j in range(1, heads):
+        value = value + ms_buf[j].astype(jnp.float32)
+    rounded = (tok + value).astype(jnp.bfloat16)
+    resid[...] = rounded.astype(jnp.float32)
+    rs_buf[me_s] = rounded
+    c_rs = state_send(4, rs_buf.at[me_s], rs_buf.at[me_s])
+    pending += c_rs
+    recv(c_rs)
+    rows = [rs_buf[j].astype(jnp.float32) for j in range(states)]
+    square = jnp.sum(rows[0] * rows[0], axis=1, keepdims=True)
+    for j in range(1, states):
+        square = square + jnp.sum(rows[j] * rows[j], axis=1, keepdims=True)
+    inv_second = lax.rsqrt(square / model + NORM_EPS)
+    logits = None
+    for j in range(states):
+        cols = pl.ds(j * width, width)
+        scaled = rows[j] * v_mn[:, cols]
+        xn[:, cols] = (scaled * inv_second).astype(jnp.bfloat16)
+        term = jnp.dot(scaled, v_rw[cols, :], precision=lax.Precision.HIGHEST, preferred_element_type=jnp.float32)
+        logits = term if logits is None else logits + term
+    logits = logits * inv_second
+    names = lax.broadcasted_iota(jnp.int32, logits.shape, 1).astype(jnp.float32)
+    hits = [names == route[:, k : k + 1] for k in range(TOPK)]
+    kept = [route[:, TOPK + k : TOPK + k + 1] < CAP for k in range(TOPK)]
+    chosen = [jnp.sum(jnp.where(hits[k], logits, 0.0), axis=1, keepdims=True) for k in range(TOPK)]
+    token_weight = jnp.zeros_like(logits)
+    loads_te = jnp.zeros_like(logits)
+    for k in range(TOPK):
+        gate_prob = 1.0 / (1.0 + jnp.exp(chosen[1 - k] - chosen[k]))
+        token_weight = token_weight + jnp.where(hits[k] & kept[k], gate_prob, 0.0)
+        loads_te = loads_te + jnp.where(hits[k] & kept[k], 1.0, 0.0)
+    load_sum = jnp.sum(loads_te, axis=0, keepdims=True)
+    load[...] = load_sum
+    prob_mean = jnp.sum(1.0 / (1.0 + jnp.exp(-logits)), axis=0, keepdims=True) / batch
+    aux[...] = experts * jnp.sum(load_sum / (batch * TOPK) * prob_mean, axis=1, keepdims=True)
+    weights = []
+    ids = lax.broadcasted_iota(jnp.int32, logits.shape, 1)
+    for e in range(local):
+        weights.append(jnp.sum(jnp.where(ids == (me_h * local + e) // split, token_weight, 0.0), axis=1, keepdims=True))
+    part = v_wg.shape[2]
+    hb = 256 if part % 256 == 0 else 128
+    for e in range(local):
+        ex_copies[e][0].wait()
+        ex_copies[e][1].wait()
+
+        def hidden_step(i, carry):
+            cols = pl.ds(pl.multiple_of(i * hb, hb), hb)
+            gate_val = dot(xn[...], v_wg[e, :, cols])
+            up_val = dot(xn[...], v_wu[e, :, cols])
+            hid[e, :, cols] = (gate_val / (1.0 + jnp.exp(-gate_val)) * up_val).astype(jnp.bfloat16)
+            return carry
+
+        lax.fori_loop(0, part // hb, hidden_step, 0)
+    for e in range(local):
+        ex_copies[e][2].wait()
+    c_x = []
+    for ds in range(states):
+        dest_s = lax.rem(me_s + ds + 1, states)
+        cols = pl.ds(pl.multiple_of(dest_s * width, width), width)
+        mix = None
+        for e in range(local):
+            term = weights[e] * dot(hid[e], v_wd[e, :, cols])
+            mix = term if mix is None else mix + term
+        for h in range(heads):
+            xo_buf[ds * heads + h] = mix[h * own : (h + 1) * own].astype(xo_buf.dtype)
+        slot = me_s * heads + me_h
+        for dh in range(1, heads + 1):
+            dest_h = lax.rem(me_h + dh, heads)
+            if ds == states - 1 and dh == heads:
+                continue
+            c = pltpu.make_async_remote_copy(
+                src_ref=xo_buf.at[ds * heads + dest_h],
+                dst_ref=xi_buf.at[slot],
+                send_sem=x_send.at[ds * heads + dh - 1],
+                recv_sem=x_recv.at[ds * heads + dh - 1],
+                device_id={"head": dest_h, "state": dest_s},
+                device_id_type=pl.DeviceIdType.MESH,
+            )
+            c.start()
+            c_x.append(c)
+    xi_buf[me_s * heads + me_h] = xo_buf[(states - 1) * heads + me_h]
+    base = jnp.zeros(out.shape, jnp.float32)
+    for h in range(heads):
+        base = base + jnp.where(me_h == h, resid[h * own : (h + 1) * own], 0.0)
+    recv(c_x)
+    mix = xi_buf[0].astype(jnp.float32)
+    for j in range(1, heads * states):
+        mix = mix + xi_buf[j].astype(jnp.float32)
+    out[...] = (base + mix).astype(jnp.bfloat16)
+    for c in pending + c_x:
+        c.wait_send()
+    for c in out_copies:
+        c.wait()
+
+
+def fused_device(tokens, mixer_norm, input_proj, conv_weight, conv_bias, conv_state, state_proj, step_gain, step_proj, step_bias, decay_log, skip_gain, ssm_state, output_proj, moe_norm, router_weight, expert_ids, slot_ids, gate_proj, up_proj, down_proj):
+    heads = lax.axis_size("head")
+    states = lax.axis_size("state")
+    own, width = tokens.shape
+    batch = own * heads
+    local, model, part = gate_proj.shape
+    experts = router_weight.shape[1]
+    split = heads * local // experts
+    slab = decay_log.shape[0]
+    chans = conv_bias.shape[0]
+    lanes = 128
+    route = jnp.concatenate([expert_ids, slot_ids], axis=1).astype(jnp.bfloat16)
+    route = jnp.pad(route, ((0, 0), (0, lanes - route.shape[1])))
+    pay = jnp.concatenate([tokens, route], axis=1)
+    mine = jnp.arange(batch)[:, None] // own == lax.axis_index("head")
+    pay = jnp.where(mine, jnp.tile(pay, (heads, 1)), 0)
+    row = lambda a: a.reshape(1, -1)
+    args = [pay, row(mixer_norm), input_proj, conv_weight, row(conv_bias), conv_state, state_proj, row(step_gain), step_proj, row(step_bias), decay_log, row(skip_gain), ssm_state, output_proj, row(moe_norm), router_weight, gate_proj, up_proj, down_proj]
+    f32, bf16 = jnp.float32, jnp.bfloat16
+    order = [1, 2, 3, 4, 5, 6, 7, 8, 9, 10, 11, 12, 13, 14, 15, 16, 17, 18]
+    scratch = [pltpu.VMEM(args[i].shape, args[i].dtype) for i in order]
+    scratch += [
+        pltpu.VMEM((heads,) + pay.shape, bf16),
+        pltpu.VMEM((states, batch, lanes), f32),
+        pltpu.VMEM((2, states, batch, chans), bf16),
+        pltpu.VMEM((heads, batch, state_proj.shape[1]), f32),
+        pltpu.VMEM((states, batch, chans), bf16),
+        pltpu.VMEM((heads, batch, width), bf16),
+        pltpu.VMEM((states, batch, width), bf16),
+        pltpu.VMEM((heads * states, own, width), f32),
+        pltpu.VMEM((heads * states, own, width), f32),
+        pltpu.VMEM((batch, chans), f32),
+        pltpu.VMEM((batch, chans), f32),
+        pltpu.VMEM((batch, chans), f32),
+        pltpu.VMEM((batch, width), f32),
+        pltpu.VMEM((batch, model), bf16),
+        pltpu.VMEM((local, batch, part), bf16),
+        pltpu.SemaphoreType.DMA((14,)),
+        pltpu.SemaphoreType.DMA((3 * local,)),
+        pltpu.SemaphoreType.DMA((2,)),
+        pltpu.SemaphoreType.DMA((3, heads)),
+        pltpu.SemaphoreType.DMA((3, heads)),
+        pltpu.SemaphoreType.DMA((5, states)),
+        pltpu.SemaphoreType.DMA((5, states)),
+        pltpu.SemaphoreType.DMA((heads * states,)),
+        pltpu.SemaphoreType.DMA((heads * states,)),
+        pltpu.SemaphoreType.DMA((conv_state.shape[0] + 1,)),
+    ]
+    anywhere = pl.BlockSpec(memory_space=pl.ANY)
+    vmem = pl.BlockSpec(memory_space=pltpu.VMEM)
+    layer_out, new_conv, new_state, load, aux = pl.pallas_call(
+        lambda *refs: fused_kernel((heads, states, own, local, split, slab), *refs),
+        out_shape=[
+            jax.ShapeDtypeStruct(tokens.shape, bf16),
+            jax.ShapeDtypeStruct(conv_state.shape, f32),
+            jax.ShapeDtypeStruct(ssm_state.shape, f32),
+            jax.ShapeDtypeStruct((1, experts), f32),
+            jax.ShapeDtypeStruct((1, 1), f32),
+        ],
+        in_specs=[vmem] + [anywhere] * 18,
+        out_specs=[vmem, anywhere, anywhere, vmem, vmem],
+        scratch_shapes=scratch,
+        compiler_params=pltpu.CompilerParams(collective_id=0, has_side_effects=True, vmem_limit_bytes=VMEM_BYTES),
+        name="decode",
+    )(*args)
+    return (layer_out, new_conv, new_state, load.reshape(-1), aux.reshape(1))
+
+
+def per_device_any(*args):
+    gate_proj = args[18]
+    batch = args[0].shape[0] * lax.axis_size("head")
+    held = sum(args[i].size * args[i].dtype.itemsize for i in (2, 6, 8, 12, 13, 18, 19, 20))
+    if batch <= 64 and gate_proj.shape[2] % 128 == 0 and held < VMEM_BYTES * 7 // 8:
+        return fused_device(*args)
+    return per_device(*args)
+
+
 def solution(mesh):
     return jax.shard_map(
-        per_device,
+        per_device_any,
         mesh=mesh,
         in_specs=(
             P(("groups", "head"), "state"),

time: 227 us -> 61.3 us (0.27)
  waiting for transfers between devices: 78.8 us -> 0 us
  blocking collectives: 77.1 us -> 0 us
  Pallas kernels: 0 us -> 44.9 us
  matrix products: 27.5 us -> 0 us
  between operations: 16.4 us -> 2.41 us
  other arithmetic: 12.6 us -> 2.76 us
  starting transfers between devices: 6.69 us -> 0 us
  local copies, waits for them, and re-layouts: 6.69 us -> 10.8 us
    psum x2 -> x0, waiting for transfers between devices: 55.1 us -> none  [the longest x1 27.6 us: per_device(): branch_full = lax.psum(branch_part, 'state')]
    pallas_call x0 -> x1, Pallas kernels: none -> 44.9 us  [fused_device(): pl.pallas_call(lambda *refs: fused_kernel((heads, states, own, local, spl...]
    psum x3 -> x0, blocking collectives: 39.5 us -> none  [the longest x1 19 us: per_device(): projected = lax.psum(proj_part, 'head')]
    dot_general x10 -> x0, matrix products: 27.5 us -> none  [the longest x1 7.47 us: expert_ffn(): jnp.einsum('nlcd,ldf->nlcf', received, up_proj, preferred_element_type=jn...]
    unnamed x1 -> x0, blocking collectives: 19 us -> none
    all_gather x2 -> x0, blocking collectives: 18.6 us -> none  [the longest x1 13.4 us: per_device(): lax.all_gather(normed, 'head', axis=0, tiled=True)]
    unnamed x4 -> x0, waiting for transfers between devices: 18.2 us -> none
    unnamed x20 -> x7, local copies, waits for them, and re-layouts: 3.35 us -> 10.8 us
  transfers between devices with their start and end apart: 5 -> 0, of which waited for: 4 -> 0; matrix products, arithmetic and copies ran while one was open for 3% -> 0% of each run, Pallas kernels for 0% -> 0%
where the time goes in v1:
time: 61.3 us; the launch traced here: 60.9 us
  Pallas kernels  44.9 us (73%)
  local copies, waits for them, and re-layouts  10.8 us (18%)
  other arithmetic  2.76 us (5%)
  between operations  2.41 us (4%)
    pallas_call x1, Pallas kernels, fused_device(): pl.pallas_call(lambda *refs: fused_kernel((heads, states, own, local, spl...  44.9 us
    unnamed x7, local copies, waits for them, and re-layouts  10.8 us
    another operation x2, other arithmetic  1.37 us

profile of v1, /device:TPU:0, one launch (start us, length us, event | category | flops | bytes accessed | tf_op | source)
XLA Modules:
  0.0 60.9 jit_solution(6589624570781444987)
XLA Ops:
  0.6 0.7 %convert.6 = bf16[4,2]{0,1:T(2,128)(2,1)S(1)} convert(s32[4,2]{0,1:T(2,128)} %param.37) | non-fusion elementwise | flops 8 | bytes 48 | tf_op jit(solution)/shard_map/convert
  1.3 0.7 %convert.7 = bf16[4,2]{0,1:T(2,128)(2,1)S(1)} convert(s32[4,2]{0,1:T(2,128)} %param.38) | non-fusion elementwise | flops 8 | bytes 48 | tf_op jit(solution)/shard_map/convert.1
  2.0 0.1 copy.29
  2.1 0.7 %fusion.1 = bf16[4,640]{1,0:T(4,128)(2,1)S(1)} fusion(bf16[4,4]{1,0:T(4,128)(2,1)S(1)} %copy.29, bf16[4,512]{1,0:T(4,128)(2,1)} %param.21), kind=kLoop, calls=%fused_computation.3 | loop fusion | flops 15360 | bytes 9248 | tf_op jit(solution)/shard_map/concatenate | solution.py:448
  2.9 0.7 %broadcast_select_fusion.refs_0_ = bf16[16,640]{1,0:T(8,128)(2,1)} fusion(bf16[16,640]{1,0:T(8,128)(2,1)S(1)} %tile.10, pred[16]{0:T(512)(128)(4,1)S(1)} %fusion.2), kind=kLoop, calls=%fused_computation | loop fusion | flops 10240 | bytes 40976 | tf_op jit(solution)/shard_map/jit(_where)/select_n | solution.py:450
  3.5 2.2 %copy.28.refs_15_ = f32[2048,8]{1,0:T(8,128)} copy(f32[2048,8]{0,1:T(8,128)} %param.36) | data formatting | bytes 131072 | tf_op args[15]
  5.7 2.5 %copy.27.refs_6_ = bf16[2048,288]{1,0:T(8,128)(2,1)} copy(bf16[2048,288]{0,1:T(8,128)(2,1)} %param.27) | data formatting | bytes 2359296 | tf_op args[6]
  8.2 44.9 %decode.1 = (bf16[4,512]{1,0:T(4,128)(2,1)}, f32[3,16,2048]{2,1,0:T(8,128)}, f32[4,16,2048]{2,1,0:T(8,128)}, f32[1,8]{1,0:T(1,128)}, f32[1,1]{1,0:T(1,128)}) custom-call(bf16[16,640]{1,0:T(8,128)(2,1)} %broadcast_select_fusion.refs_0_, f32[1,512]{1,0:T(1,128)} %bitcast.12, bf16[2,512,2048]{2,1,0:T(8,128)(2,1)} %refs_2_.1, f32[4,2048]{1,0:T(4,128)} %refs_3_.1, ...), custom_call_target="tpu_custom_call" | custom-call | tf_op jit(solution)/shard_map/decode/pallas_call | solution.py:485
  53.1 1.3 %copy.35 = bf16[4,512]{1,0:T(4,128)(2,1)} copy(bf16[4,512]{1,0:T(4,128)(2,1)} %get-tuple-element.20) | data formatting | bytes 8192
  54.4 1.8 %copy.36 = f32[3,16,2048]{2,1,0:T(8,128)} copy(f32[3,16,2048]{2,1,0:T(8,128)} %get-tuple-element.21) | data formatting | bytes 786432
  56.2 1.9 %copy.37 = f32[4,16,2048]{2,1,0:T(8,128)} copy(f32[4,16,2048]{2,1,0:T(8,128)} %get-tuple-element.22) | data formatting | bytes 1048576
  58.0 1.1 %copy.38 = f32[8]{0:T(128)} copy(f32[8]{0:T(128)} %bitcast.14) | data formatting | bytes 64
  (4 shorter events, 0.0 us)

commit v2 on v1

--- a/solution.py
+++ b/solution.py
@@ -152,6 +152,10 @@
     return jnp.dot(left, right, preferred_element_type=jnp.float32)
 
 
+def dot_t(left, right, precision=None):
+    return lax.dot_general(left, right, (((1,), (1,)), ((), ())), precision=precision, preferred_element_type=jnp.float32)
+
+
 def fused_kernel(dims, *refs):
     heads, states, own, local, split, slab = dims
     (pay, nrm, wi, cw, cb, cs, wsp, sg, wst, sb, dl, sk, ss, wo, mn, rw, wg, wu, wd) = refs[:19]
@@ -166,7 +170,7 @@
     model = width * states
     chans = v_cb.shape[1]
     rank = v_sg.shape[1]
-    experts = v_rw.shape[1]
+    experts = v_rw.shape[0]
 
     smalls = [(nrm, v_nrm), (cw, v_cw), (cb, v_cb), (cs, v_cs), (wsp, v_wsp), (sg, v_sg), (wst, v_wst), (sb, v_sb), (dl, v_dl), (sk, v_sk), (ss, v_ss), (wo, v_wo), (mn, v_mn), (rw, v_rw)]
     in_copies = [pltpu.make_async_copy(wi.at[k], v_wi.at[k], in_sem.at[k]) for k in range(2)]
@@ -273,7 +277,7 @@
             acc = acc + v_cw[k : k + 1, cols] * v_cs[k, :, cols]
         acc = acc + v_cb[:, cols]
         conv_out[:, cols] = acc / (1.0 + jnp.exp(-acc))
-    pj_buf[me_h] = dot(conv_out[...].astype(jnp.bfloat16), v_wsp[...])
+    pj_buf[me_h] = dot_t(conv_out[...].astype(jnp.bfloat16), v_wsp[...])
     c_pj = head_send(1, pj_buf.at[me_h], pj_buf.at[me_h])
     pending += c_pj
     out_copies = [pltpu.make_async_copy(conv_in, new_conv.at[v_cs.shape[0] - 1], o_sem.at[0])]
@@ -355,7 +359,7 @@
         cols = pl.ds(j * width, width)
         scaled = rows[j] * v_mn[:, cols]
         xn[:, cols] = (scaled * inv_second).astype(jnp.bfloat16)
-        term = jnp.dot(scaled, v_rw[cols, :], precision=lax.Precision.HIGHEST, preferred_element_type=jnp.float32)
+        term = dot_t(scaled, v_rw[:, cols], lax.Precision.HIGHEST)
         logits = term if logits is None else logits + term
     logits = logits * inv_second
     names = lax.broadcasted_iota(jnp.int32, logits.shape, 1).astype(jnp.float32)
@@ -449,7 +453,7 @@
     mine = jnp.arange(batch)[:, None] // own == lax.axis_index("head")
     pay = jnp.where(mine, jnp.tile(pay, (heads, 1)), 0)
     row = lambda a: a.reshape(1, -1)
-    args = [pay, row(mixer_norm), input_proj, conv_weight, row(conv_bias), conv_state, state_proj, row(step_gain), step_proj, row(step_bias), decay_log, row(skip_gain), ssm_state, output_proj, row(moe_norm), router_weight, gate_proj, up_proj, down_proj]
+    args = [pay, row(mixer_norm), input_proj, conv_weight, row(conv_bias), conv_state, state_proj.T, row(step_gain), step_proj, row(step_bias), decay_log, row(skip_gain), ssm_state, output_proj, row(moe_norm), router_weight.T, gate_proj, up_proj, down_proj]
     f32, bf16 = jnp.float32, jnp.bfloat16
     order = [1, 2, 3, 4, 5, 6, 7, 8, 9, 10, 11, 12, 13, 14, 15, 16, 17, 18]
     scratch = [pltpu.VMEM(args[i].shape, args[i].dtype) for i in order]

time: 61.3 us -> 57.2 us (0.933)
  local copies, waits for them, and re-layouts: 10.8 us -> 6.22 us
    unnamed x7 -> x5, local copies, waits for them, and re-layouts: 10.8 us -> 6.19 us
where the time goes in v2:
time: 57.2 us; the launch traced here: 56.8 us
  Pallas kernels  45.4 us (79%)
  local copies, waits for them, and re-layouts  6.22 us (11%)
  other arithmetic  2.76 us (5%)
  between operations  2.42 us (4%)
    pallas_call x1, Pallas kernels, fused_device(): pl.pallas_call(lambda *refs: fused_kernel((heads, states, own, local, spl...  45.4 us
    unnamed x5, local copies, waits for them, and re-layouts  6.19 us
    another operation x2, other arithmetic  1.37 us

profile of v2, /device:TPU:0, one launch (start us, length us, event | category | flops | bytes accessed | tf_op | source)
XLA Modules:
  0.0 56.8 jit_solution(10722624085482201743)
XLA Ops:
  0.6 0.7 %convert.6 = bf16[4,2]{0,1:T(2,128)(2,1)S(1)} convert(s32[4,2]{0,1:T(2,128)} %param.37) | non-fusion elementwise | flops 8 | bytes 48 | tf_op jit(solution)/shard_map/convert
  1.3 0.7 %convert.7 = bf16[4,2]{0,1:T(2,128)(2,1)S(1)} convert(s32[4,2]{0,1:T(2,128)} %param.38) | non-fusion elementwise | flops 8 | bytes 48 | tf_op jit(solution)/shard_map/convert.1
  2.0 0.1 copy.27
  2.1 0.7 %fusion.1 = bf16[4,640]{1,0:T(4,128)(2,1)S(1)} fusion(bf16[4,4]{1,0:T(4,128)(2,1)S(1)} %copy.27, bf16[4,512]{1,0:T(4,128)(2,1)} %param.21), kind=kLoop, calls=%fused_computation.3 | loop fusion | flops 15360 | bytes 9248 | tf_op jit(solution)/shard_map/concatenate | solution.py:452
  2.9 0.7 %broadcast_select_fusion.refs_0_ = bf16[16,640]{1,0:T(8,128)(2,1)} fusion(bf16[16,640]{1,0:T(8,128)(2,1)S(1)} %tile.10, pred[16]{0:T(512)(128)(4,1)S(1)} %fusion.2), kind=kLoop, calls=%fused_computation | loop fusion | flops 10240 | bytes 40976 | tf_op jit(solution)/shard_map/jit(_where)/select_n | solution.py:454
  3.5 45.4 %decode.1 = (bf16[4,512]{1,0:T(4,128)(2,1)}, f32[3,16,2048]{2,1,0:T(8,128)}, f32[4,16,2048]{2,1,0:T(8,128)}, f32[1,8]{1,0:T(1,128)}, f32[1,1]{1,0:T(1,128)}) custom-call(bf16[16,640]{1,0:T(8,128)(2,1)} %broadcast_select_fusion.refs_0_, f32[1,512]{1,0:T(1,128)} %bitcast.16, bf16[2,512,2048]{2,1,0:T(8,128)(2,1)} %refs_2_.1, f32[4,2048]{1,0:T(4,128)} %refs_3_.1, ...), custom_call_target="tpu_custom_call" | custom-call | tf_op jit(solution)/shard_map/decode/pallas_call | solution.py:489
  48.9 1.3 %copy.33 = bf16[4,512]{1,0:T(4,128)(2,1)} copy(bf16[4,512]{1,0:T(4,128)(2,1)} %get-tuple-element.20) | data formatting | bytes 8192
  50.2 1.8 %copy.34 = f32[3,16,2048]{2,1,0:T(8,128)} copy(f32[3,16,2048]{2,1,0:T(8,128)} %get-tuple-element.21) | data formatting | bytes 786432
  52.0 1.9 %copy.35 = f32[4,16,2048]{2,1,0:T(8,128)} copy(f32[4,16,2048]{2,1,0:T(8,128)} %get-tuple-element.22) | data formatting | bytes 1048576
  53.8 1.2 %copy.36 = f32[8]{0:T(128)} copy(f32[8]{0:T(128)} %bitcast.18) | data formatting | bytes 64
  (4 shorter events, 0.0 us)
